TPU v7x, 32 devices: a whole 2x2x4 slice. The times are simulated.
32 devices in a mesh: rep: 2 (over x), fsdp: 16 (over z, y, core).
Axes of the slice: x: 2, y: 2, z: 4, core: 2. Of those that a mesh axis runs over, the one named last changes fastest.
Arguments:
- tokens: bfloat16 [256, 3584], P(('rep', 'fsdp')), may hold values from -6 to 6
- targets: bfloat16 [256, 3584], P(('rep', 'fsdp')), may hold values from -6 to 6
- gate_weight: bfloat16 [3584, 18944], P(None, 'fsdp'), may hold values from -0.09375 to 0.09375
- up_weight: bfloat16 [3584, 18944], P(None, 'fsdp'), may hold values from -0.09375 to 0.09375
- down_weight: bfloat16 [18944, 3584], P('fsdp'), may hold values from -0.046875 to 0.046875
- gate_direction: bfloat16 [3584, 18944], P(None, 'fsdp'), may hold values from -0.09375 to 0.09375
- up_direction: bfloat16 [3584, 18944], P(None, 'fsdp'), may hold values from -0.09375 to 0.09375
- down_direction: bfloat16 [18944, 3584], P('fsdp'), may hold values from -0.046875 to 0.046875
Outputs:
- hvp_gate: float32 [3584, 18944], P(None, 'fsdp')
- hvp_up: float32 [3584, 18944], P(None, 'fsdp')
- hvp_down: float32 [18944, 3584], P('fsdp')
All inputs are finite; a program needn't handle non-finite values.
Results may differ from a plain program's by a relative error of at most 0.0069.
Values may be sent and summed in bfloat16 or wider, within the bound.
A program may use at most 192 MiB of HBM per device.

v0:
```python
import jax
import jax.numpy as jnp
from jax import lax
from jax.sharding import PartitionSpec as P


def silu_parts(gate):
    sigmoid_value = jax.nn.sigmoid(gate)
    slope = sigmoid_value * (1.0 + gate * (1.0 - sigmoid_value))
    bend = sigmoid_value * (1.0 - sigmoid_value) * (2.0 + gate * (1.0 - 2.0 * sigmoid_value))
    return (gate * sigmoid_value, slope, bend)


def inner_rows(left, right):
    return lax.dot_general(
        left, right, (((0,), (0,)), ((), ())), preferred_element_type=jnp.float32
    )


def products(
    gathered,
    gate_grad_tangent,
    up_grad_tangent,
    hidden,
    hidden_tangent,
    error_all,
    error_tangent_all,
):
    hvp_gate = inner_rows(gathered, gate_grad_tangent)
    hvp_up = inner_rows(gathered, up_grad_tangent)
    hvp_down = inner_rows(hidden_tangent, error_all) + inner_rows(hidden, error_tangent_all)
    return (hvp_gate, hvp_up, hvp_down)


def on_device(
    tokens,
    targets,
    gate_weight,
    up_weight,
    down_weight,
    gate_direction,
    up_direction,
    down_direction,
):
    width = tokens.shape[1]
    gathered = lax.all_gather(tokens, "fsdp", axis=0, tiled=True)
    gate = jnp.dot(gathered, gate_weight, preferred_element_type=jnp.float32)
    up = jnp.dot(gathered, up_weight, preferred_element_type=jnp.float32)
    gate_tangent = jnp.dot(gathered, gate_direction, preferred_element_type=jnp.float32)
    up_tangent = jnp.dot(gathered, up_direction, preferred_element_type=jnp.float32)
    activation, slope, bend = silu_parts(gate)
    hidden = (activation * up).astype(jnp.bfloat16)
    hidden_tangent = (slope * gate_tangent * up + activation * up_tangent).astype(jnp.bfloat16)
    primal = jnp.dot(hidden, down_weight, preferred_element_type=jnp.float32)
    tangent = jnp.dot(hidden_tangent, down_weight, preferred_element_type=jnp.float32) + jnp.dot(
        hidden, down_direction, preferred_element_type=jnp.float32
    )
    summed = lax.psum_scatter(
        jnp.concatenate([primal, tangent], axis=1), "fsdp", scatter_dimension=0, tiled=True
    )
    error = (summed[:, :width] - targets.astype(jnp.float32)).astype(jnp.bfloat16)
    error_tangent = summed[:, width:].astype(jnp.bfloat16)
    error_all, error_tangent_all = (
        lax.all_gather(error, "fsdp", axis=0, tiled=True),
        lax.all_gather(error_tangent, "fsdp", axis=0, tiled=True),
    )
    back = jnp.dot(error_all, down_weight.T, preferred_element_type=jnp.float32)
    back_tangent = jnp.dot(
        error_tangent_all, down_weight.T, preferred_element_type=jnp.float32
    ) + jnp.dot(error_all, down_direction.T, preferred_element_type=jnp.float32)
    gate_grad_tangent = (
        back_tangent * up * slope + back * up_tangent * slope + back * up * bend * gate_tangent
    ).astype(jnp.bfloat16)
    up_grad_tangent = (back_tangent * activation + back * slope * gate_tangent).astype(jnp.bfloat16)
    pair_rows = (
        lax.all_gather(gathered, "rep", axis=0, tiled=True),
        lax.all_gather(gate_grad_tangent, "rep", axis=0, tiled=True),
        lax.all_gather(up_grad_tangent, "rep", axis=0, tiled=True),
        lax.all_gather(hidden, "rep", axis=0, tiled=True),
        lax.all_gather(hidden_tangent, "rep", axis=0, tiled=True),
        lax.all_gather(error_all, "rep", axis=0, tiled=True),
        lax.all_gather(error_tangent_all, "rep", axis=0, tiled=True),
    )
    hvp_gate, hvp_up, hvp_down = products(
        pair_rows[0],
        pair_rows[1],
        pair_rows[2],
        pair_rows[3],
        pair_rows[4],
        pair_rows[5],
        pair_rows[6],
    )
    return (hvp_gate, hvp_up, hvp_down)


def solution(mesh):
    in_specs = (
        P(("rep", "fsdp"), None),
        P(("rep", "fsdp"), None),
        P(None, "fsdp"),
        P(None, "fsdp"),
        P("fsdp", None),
        P(None, "fsdp"),
        P(None, "fsdp"),
        P("fsdp", None),
    )
    out_specs = (P(None, "fsdp"), P(None, "fsdp"), P("fsdp", None))
    return jax.shard_map(
        on_device, mesh=mesh, in_specs=in_specs, out_specs=out_specs, check_vma=False
    )
```

profile of v0, /device:TPU:0, one launch (start us, length us, event | category | flops | bytes accessed | tf_op | source)
XLA Modules:
  0.0 296.1 jit_solution(9094616543245920694)
XLA Ops:
  8.0 0.0 reduce-scatter.2.cloned.1.call-start
  8.0 26.1 %all_gather.30 = bf16[128,3584]{1,0:T(8,128)(2,1)S(1)} all-gather(bf16[8,3584]{1,0:T(8,128)(2,1)} %param.8), channel_id=1, replica_groups=mesh['rep'=2,'fsdp'=16] {'fsdp'}, dimensions={0}, use_global_device_ids=true | all-gather | bytes 974848 | tf_op jit(solution)/shard_map/all_gather | solution.py:46
  34.2 6.1 %fusion.12 = f32[128,1184]{0,1:T(8,128)S(1)} fusion(bf16[128,3584]{1,0:T(8,128)(2,1)S(1)} %all_gather.30, bf16[3584,1184]{0,1:T(8,128)(2,1)} %param.14), kind=kOutput, calls=%fused_computation.26 | convolution fusion | flops 1086324736 | bytes 10010624 | tf_op jit(solution)/shard_map/dot_general | solution.py:50
  40.4 0.0 copy-done.1
  40.4 0.0 copy-start.5
  40.4 0.0 slice-start.8
  40.4 0.0 slice-start.9
  40.4 0.0 slice-start.10
  40.4 2.4 fusion.11
  42.8 0.0 slice-done.6
  42.8 0.2 slice-done.7
  43.0 0.1 slice-done.8
  43.0 2.4 fusion.9
  45.4 0.0 copy-done
  45.4 0.0 copy-done.5
  45.4 0.0 copy-done.7
  45.4 0.0 slice-done.9
  45.4 0.4 slice-done.10
  45.8 0.0 slice-done.11
  45.8 3.3 %multiply_convert_fusion = (bf16[128,1184]{0,1:T(8,128)(2,1)S(1)}, bf16[128,1184]{0,1:T(8,128)(2,1)S(1)}, f32[128,1184]{0,1:T(8,128)}) fusion(f32[128,1184]{0,1:T(8,128)S(1)} %fusion.9, f32[128,1184]{0,1:T(8,128)S(1)} %fusion.12, f32[128,1184]{0,1:T(8,128)S(1)} %fusion.11, bf16[128,3584]{1,0:T(8,128)(2,1)S(1)} %all_gather.30, ...), kind=kOutput, calls=%fused_computation.17 | convolution fusion | flops 1088598016 | bytes 12435456 | tf_op jit(solution)/shard_map/dot_general | solution.py:48
  49.1 0.0 copy-done.9
  49.1 0.0 slice-done
  49.1 0.0 slice-done.1
  49.1 0.0 slice-done.2
  49.1 0.0 slice-start.3
  49.1 0.0 slice-start.4
  49.1 1.4 fusion.13
  50.5 0.0 slice-start.5
  50.5 1.4 fusion.10
  51.9 0.0 slice-done.3
  51.9 0.7 slice-done.4
  52.6 0.1 slice-done.5
  52.6 1.4 convolution_add_fusion.1
  54.0 0.0 copy-start.12
  54.0 2.1 pad_maximum_fusion
  56.1 0.0 reduce-scatter.2.cloned.1.call-update
  56.1 0.0 all-gather.4.cloned.1.call-start
  56.2 0.5 all-gather.4.cloned.1.call-update
  56.7 0.0 all-gather.6.cloned.1.call-start
  56.8 65.3 %reduce-scatter.2.cloned.1.call-done = f32[8,7168]{1,0:T(8,128)} async-done(((f32[128,7168]{1,0:T(8,128)}), f32[8,7168]{1,0:T(8,128)}) %reduce-scatter.2.cloned.1.call-update) | async-done | bytes 229392 | tf_op jit(solution)/shard_map/reduce_scatter | solution.py:58
  122.1 0.0 copy-done.12
  122.1 0.9 fusion.8
  123.0 23.4 %all_gather.32 = bf16[128,3584]{1,0:T(8,128)(2,1)} all-gather(bf16[8,3584]{1,0:T(8,128)(2,1)S(1)} %fusion.8), channel_id=1, replica_groups=mesh['rep'=2,'fsdp'=16] {'fsdp'}, dimensions={0}, use_global_device_ids=true | all-gather | bytes 974848 | tf_op jit(solution)/shard_map/all_gather | solution.py:64
  146.4 0.0 all-gather.6.cloned.1.call-update
  146.4 0.0 all-gather.8.cloned.1.call-start
  146.4 13.5 %all_gather.36 = bf16[256,1184]{0,1:T(8,128)(2,1)S(1)} all-gather(bf16[128,1184]{0,1:T(8,128)(2,1)S(1)} %get-tuple-element.6), channel_id=1, replica_groups=mesh['rep'=2,'fsdp'=16] {'rep'}, dimensions={0}, use_global_device_ids=true | all-gather | bytes 909312 | tf_op jit(solution)/shard_map/all_gather | solution.py:80
  159.9 17.0 %all_gather.38 = bf16[256,1184]{0,1:T(8,128)(2,1)S(1)} all-gather(bf16[128,1184]{0,1:T(8,128)(2,1)S(1)} %get-tuple-element.5), channel_id=1, replica_groups=mesh['rep'=2,'fsdp'=16] {'rep'}, dimensions={0}, use_global_device_ids=true | all-gather | bytes 909312 | tf_op jit(solution)/shard_map/all_gather | solution.py:79
  176.9 0.9 slice.15
  177.8 20.2 %all_gather.31 = bf16[128,3584]{1,0:T(8,128)(2,1)S(1)} all-gather(bf16[8,3584]{1,0:T(8,128)(2,1)S(1)} %slice.15), channel_id=1, replica_groups=mesh['rep'=2,'fsdp'=16] {'fsdp'}, dimensions={0}, use_global_device_ids=true | all-gather | bytes 974848 | tf_op jit(solution)/shard_map/all_gather | solution.py:65
  198.1 7.0 %fusion.14 = f32[128,1184]{0,1:T(8,128)} fusion(bf16[128,3584]{1,0:T(8,128)(2,1)S(1)} %all_gather.31, bf16[1184,3584]{1,0:T(8,128)(2,1)} %param.12), kind=kOutput, calls=%fused_computation.28 | convolution fusion | flops 1086324736 | bytes 10010624 | tf_op jit(solution)/shard_map/dot_general | solution.py:68
  205.0 0.0 all-gather.8.cloned.1.call-update
  205.1 0.0 copy-start.8
  205.1 6.0 %convolution_add_fusion.2 = f32[128,1184]{0,1:T(8,128)S(1)} fusion(f32[128,1184]{0,1:T(8,128)} %fusion.14, bf16[128,3584]{1,0:T(8,128)(2,1)S(1)} %copy-done.3, bf16[1184,3584]{1,0:T(8,128)(2,1)} %param.15), kind=kOutput, calls=%fused_computation.5 | convolution fusion | flops 1086476288 | bytes 10616832 | tf_op jit(solution)/shard_map/dot_general | solution.py:70
  211.1 0.0 copy-done.6
  211.1 0.0 copy-done.8
  211.1 0.0 copy-done.10
  211.1 0.0 copy-done.11
  211.2 6.4 %add_convert_fusion = (bf16[128,1184]{0,1:T(8,128)(2,1)S(1)}, bf16[128,1184]{0,1:T(8,128)(2,1)S(1)}) fusion(f32[128,1184]{0,1:T(8,128)S(1)} %copy-done.8, f32[128,1184]{0,1:T(8,128)S(1)} %convolution_add_fusion.2, f32[128,1184]{0,1:T(8,128)S(1)} %copy-done.10, f32[128,1184]{0,1:T(8,128)S(1)} %copy-done.11, f32[128,1184]{0,1:T(8,128)S(1)} %copy-done.6, ...), kind=kOutput, calls=%fused_computation.15 | convolution fusion | flops 1090568192 | bytes 13041664 | tf_op jit(solution)/shard_map/dot_general | solution.py:67
  217.6 17.2 %all_gather.33 = bf16[256,1184]{0,1:T(8,128)(2,1)S(1)} all-gather(bf16[128,1184]{0,1:T(8,128)(2,1)S(1)} %get-tuple-element.4), channel_id=1, replica_groups=mesh['rep'=2,'fsdp'=16] {'rep'}, dimensions={0}, use_global_device_ids=true | all-gather | bytes 909312 | tf_op jit(solution)/shard_map/all_gather | solution.py:77
  234.7 10.2 %convolution_bitcast_fusion.1 = f32[3584,1184]{0,1:T(8,128)} fusion(bf16[256,1184]{0,1:T(8,128)(2,1)S(1)} %all_gather.33, bf16[256,3584]{1,0:T(8,128)(2,1)} %all-gather.4.cloned.1.call-done), kind=kOutput, calls=%fused_computation.2 | convolution fusion | flops 2172649472 | bytes 19415040 | tf_op jit(solution)/shard_map/dot_general | solution.py:15
  245.0 9.9 %all_gather.35 = bf16[256,1184]{0,1:T(8,128)(2,1)S(1)} all-gather(bf16[128,1184]{0,1:T(8,128)(2,1)S(1)} %get-tuple-element.3), channel_id=1, replica_groups=mesh['rep'=2,'fsdp'=16] {'rep'}, dimensions={0}, use_global_device_ids=true | all-gather | bytes 909312 | tf_op jit(solution)/shard_map/all_gather | solution.py:78
  254.9 8.6 %convolution_bitcast_fusion = f32[3584,1184]{0,1:T(8,128)} fusion(bf16[256,1184]{0,1:T(8,128)(2,1)S(1)} %all_gather.35, bf16[256,3584]{1,0:T(8,128)(2,1)S(1)} %copy-done.4), kind=kOutput, calls=%fused_computation.1 | convolution fusion | flops 2172649472 | bytes 19415040 | tf_op jit(solution)/shard_map/dot_general | solution.py:15
  263.5 10.1 %fusion.15 = f32[1184,3584]{1,0:T(8,128)} fusion(bf16[256,1184]{0,1:T(8,128)(2,1)S(1)} %all_gather.36, bf16[256,3584]{1,0:T(8,128)(2,1)} %all-gather.6.cloned.1.call-done), kind=kOutput, calls=%fused_computation.29 | convolution fusion | flops 2172649472 | bytes 19415040 | tf_op jit(solution)/shard_map/dot_general | solution.py:15
  273.6 15.0 %convolution_add_fusion = f32[1184,3584]{1,0:T(8,128)} fusion(f32[1184,3584]{1,0:T(8,128)} %fusion.15, bf16[256,1184]{0,1:T(8,128)(2,1)S(1)} %all_gather.38, bf16[256,3584]{1,0:T(8,128)(2,1)} %all-gather.8.cloned.1.call-done), kind=kOutput, calls=%fused_computation | convolution fusion | flops 2176892928 | bytes 36388864 | tf_op jit(solution)/shard_map/dot_general | solution.py:15
  (26 shorter events, 0.0 us)
Async XLA Ops:
  8.0 114.1 %reduce-scatter.2.cloned.1.call-start = ((), (), s32[]{:S(2)}) async-start(), calls=%async_computation.1 | async-start | bytes 3899392 | tf_op jit(solution)/shard_map/reduce_scatter | solution.py:58
  34.2 11.2 %copy-start = (bf16[128,3584]{1,0:T(8,128)(2,1)}, bf16[128,3584]{1,0:T(8,128)(2,1)S(1)}, u32[]{:S(2)}) copy-start(bf16[128,3584]{1,0:T(8,128)(2,1)S(1)} %all_gather.30) | copy-start | bytes 2752516
  34.2 6.2 %copy-start.1 = (bf16[3584,1184]{0,1:T(8,128)(2,1)S(1)}, bf16[3584,1184]{0,1:T(8,128)(2,1)}, u32[]{:S(2)}) copy-start(bf16[3584,1184]{0,1:T(8,128)(2,1)} %param.13) | copy-start | bytes 25460740
  34.2 8.6 %slice-start.6 = ((s8[8486912]{0:T(1024)(128)(4,1)}), s8[4194304]{0:T(1024)(128)(4,1)S(1)}, s32[]{:S(2)}) async-start(s8[8486912]{0:T(1024)(128)(4,1)} %bitcast.36), calls=%async_computation.11 | async-start | bytes 8388608
  34.2 8.8 %slice-start.7 = ((s8[8486912]{0:T(1024)(128)(4,1)}), s8[4194304]{0:T(1024)(128)(4,1)S(1)}, s32[]{:S(2)}) async-start(s8[8486912]{0:T(1024)(128)(4,1)} %bitcast.36), calls=%async_computation.12 | async-start | bytes 8388608
  40.4 5.0 %copy-start.5 = (f32[128,1184]{0,1:T(8,128)}, f32[128,1184]{0,1:T(8,128)S(1)}, u32[]{:S(2)}) copy-start(f32[128,1184]{0,1:T(8,128)S(1)} %fusion.12) | copy-start | bytes 1818628
  40.4 2.6 slice-start.8
  40.4 5.0 %slice-start.9 = ((s8[8486912]{0:T(1024)(128)(4,1)}), s8[4194304]{0:T(1024)(128)(4,1)S(1)}, s32[]{:S(2)}) async-start(s8[8486912]{0:T(1024)(128)(4,1)} %bitcast.38), calls=%async_computation.14 | async-start | bytes 8388608
  40.4 5.4 %slice-start.10 = ((s8[8486912]{0:T(1024)(128)(4,1)}), s8[4194304]{0:T(1024)(128)(4,1)S(1)}, s32[]{:S(2)}) async-start(s8[8486912]{0:T(1024)(128)(4,1)} %bitcast.38), calls=%async_computation.15 | async-start | bytes 8388608
  43.0 2.4 copy-start.7
  43.0 2.8 slice-start.11
  43.0 6.0 %slice-start = ((s8[8486912]{0:T(1024)(128)(4,1)}), s8[4194304]{0:T(1024)(128)(4,1)S(1)}, s32[]{:S(2)}) async-start(s8[8486912]{0:T(1024)(128)(4,1)} %bitcast.32), calls=%async_computation.5 | async-start | bytes 8388608
  43.0 6.0 %slice-start.1 = ((s8[8486912]{0:T(1024)(128)(4,1)}), s8[4194304]{0:T(1024)(128)(4,1)S(1)}, s32[]{:S(2)}) async-start(s8[8486912]{0:T(1024)(128)(4,1)} %bitcast.32), calls=%async_computation.6 | async-start | bytes 8388608
  45.8 3.3 %copy-start.9 = (f32[128,1184]{0,1:T(8,128)}, f32[128,1184]{0,1:T(8,128)S(1)}, u32[]{:S(2)}) copy-start(f32[128,1184]{0,1:T(8,128)S(1)} %fusion.9) | copy-start | bytes 1818628
  45.8 3.3 %slice-start.2 = ((s8[8486912]{0:T(1024)(128)(4,1)}), s8[98304]{0:T(1024)(128)(4,1)S(1)}, s32[]{:S(2)}) async-start(s8[8486912]{0:T(1024)(128)(4,1)} %bitcast.32), calls=%async_computation.7 | async-start | bytes 196608
  49.1 2.8 slice-start.3
  49.1 3.5 %slice-start.4 = ((s8[8486912]{0:T(1024)(128)(4,1)}), s8[4194304]{0:T(1024)(128)(4,1)S(1)}, s32[]{:S(2)}) async-start(s8[8486912]{0:T(1024)(128)(4,1)} %bitcast.34), calls=%async_computation.9 | async-start | bytes 8388608
  50.5 2.1 slice-start.5
  54.0 68.1 %copy-start.12 = (bf16[8,3584]{1,0:T(8,128)(2,1)S(1)}, bf16[8,3584]{1,0:T(8,128)(2,1)}, u32[]{:S(2)}) copy-start(bf16[8,3584]{1,0:T(8,128)(2,1)} %param.9) | copy-start | bytes 172036
  56.1 178.6 %all-gather.4.cloned.1.call-start = ((), (), s32[]{:S(2)}) async-start(), calls=%async_computation.2 | async-start | bytes 2752512 | tf_op jit(solution)/shard_map/all_gather | solution.py:76
  56.7 206.7 %all-gather.6.cloned.1.call-start = ((), (), s32[]{:S(2)}) async-start(), calls=%async_computation.3 | async-start | bytes 2752512 | tf_op jit(solution)/shard_map/all_gather | solution.py:81
  146.4 127.2 %all-gather.8.cloned.1.call-start = ((), (), s32[]{:S(2)}) async-start(), calls=%async_computation.4 | async-start | bytes 2752512 | tf_op jit(solution)/shard_map/all_gather | solution.py:82
  198.1 7.0 %copy-start.2 = (bf16[128,3584]{1,0:T(8,128)(2,1)}, bf16[128,3584]{1,0:T(8,128)(2,1)S(1)}, u32[]{:S(2)}) copy-start(bf16[128,3584]{1,0:T(8,128)(2,1)S(1)} %all_gather.31) | copy-start | bytes 2752516
  198.1 7.0 %copy-start.3 = (bf16[128,3584]{1,0:T(8,128)(2,1)S(1)}, bf16[128,3584]{1,0:T(8,128)(2,1)}, u32[]{:S(2)}) copy-start(bf16[128,3584]{1,0:T(8,128)(2,1)} %all_gather.32) | copy-start | bytes 2752516
  205.1 6.1 %copy-start.6 = (f32[128,1184]{0,1:T(8,128)S(1)}, f32[128,1184]{0,1:T(8,128)}, u32[]{:S(2)}) copy-start(f32[128,1184]{0,1:T(8,128)} %copy-done.5) | copy-start | bytes 1818628
  205.1 6.1 %copy-start.8 = (f32[128,1184]{0,1:T(8,128)S(1)}, f32[128,1184]{0,1:T(8,128)}, u32[]{:S(2)}) copy-start(f32[128,1184]{0,1:T(8,128)} %copy-done.7) | copy-start | bytes 1818628
  205.1 6.1 %copy-start.10 = (f32[128,1184]{0,1:T(8,128)S(1)}, f32[128,1184]{0,1:T(8,128)}, u32[]{:S(2)}) copy-start(f32[128,1184]{0,1:T(8,128)} %copy-done.9) | copy-start | bytes 1818628
  205.1 6.1 %copy-start.11 = (f32[128,1184]{0,1:T(8,128)S(1)}, f32[128,1184]{0,1:T(8,128)}, u32[]{:S(2)}) copy-start(f32[128,1184]{0,1:T(8,128)} %get-tuple-element.7) | copy-start | bytes 1818628
  234.7 20.1 %copy-start.4 = (bf16[256,3584]{1,0:T(8,128)(2,1)S(1)}, bf16[256,3584]{1,0:T(8,128)(2,1)}, u32[]{:S(2)}) copy-start(bf16[256,3584]{1,0:T(8,128)(2,1)} %all-gather.4.cloned.1.call-done) | copy-start | bytes 5505028
Sparse Core Ops, SparseCore 0:
  56.3 65.7 reduce-scatter.1
Sparse Core Ops, SparseCore 1:
  58.7 27.2 all-gather.3
  146.5 36.4 all-gather.5
  205.1 35.3 all-gather.7
where the time goes:
time: 296 us
  blocking collectives  127 us (43%)
  matrix products  81.6 us (28%)
  waiting for transfers between devices  65.9 us (22%)
  between operations  15.9 us (5%)
  other arithmetic  3 us (1%)
    reduce_scatter x1, waiting for transfers between devices, on_device(): lax.psum_scatter(jnp.concatenate([primal, tangent], axis=1), 'fsdp', scat...  65.3 us
    dot_general x4, matrix products, inner_rows(): lax.dot_general(left, right, (((0,), (0,)), ((), ())), preferred_element_...  43.9 us
    all_gather x1, blocking collectives, on_device(): gathered = lax.all_gather(tokens, 'fsdp', axis=0, tiled=True)  26.1 us
    all_gather x1, blocking collectives, on_device(): lax.all_gather(error, 'fsdp', axis=0, tiled=True)  23.4 us
    all_gather x1, blocking collectives, on_device(): lax.all_gather(error_tangent, 'fsdp', axis=0, tiled=True)  20.2 us
    all_gather x1, blocking collectives, on_device(): lax.all_gather(gate_grad_tangent, 'rep', axis=0, tiled=True)  17.2 us
    all_gather x1, blocking collectives, on_device(): lax.all_gather(hidden, 'rep', axis=0, tiled=True)  17 us
    all_gather x1, blocking collectives, on_device(): lax.all_gather(hidden_tangent, 'rep', axis=0, tiled=True)  13.5 us
  transfers between devices with their start and end apart: 4, of which 1 were waited for; matrix products, arithmetic and copies ran while one was open for 17% of the time, Pallas kernels for 0%

commit v1 on v0

v1 whole, which is shorter than its diff:
```python
import functools

import jax
import jax.numpy as jnp
from jax import lax
from jax.experimental import pallas as pl
from jax.experimental.pallas import tpu as pltpu
from jax.sharding import PartitionSpec as P

MESH = pl.DeviceIdType.MESH
F32 = jnp.float32
BF16 = jnp.bfloat16


def silu_parts(gate):
    sigmoid_value = jax.nn.sigmoid(gate)
    slope = sigmoid_value * (1.0 + gate * (1.0 - sigmoid_value))
    bend = sigmoid_value * (1.0 - sigmoid_value) * (2.0 + gate * (1.0 - 2.0 * sigmoid_value))
    return (gate * sigmoid_value, slope, bend)


def inner_rows(left, right):
    return lax.dot_general(left, right, (((0,), (0,)), ((), ())), preferred_element_type=F32)


class Place:
    def __init__(self, reps, bits):
        me = lax.axis_index("fsdp")
        rep = lax.axis_index("rep")
        self.reps, self.bits = reps, bits
        self.bit = [lax.rem(me // (1 << s), 2) for s in range(bits)]
        self.partner = [me + (1 << s) * (1 - 2 * self.bit[s]) for s in range(bits)]
        self.other_rep = [lax.rem(rep + d, reps) for d in range(1, reps)]
        self.slot = sum(self.bit[s] * (1 << (bits - 1 - s)) for s in range(bits))

    def meet(self):
        barrier = pltpu.get_barrier_semaphore()
        for partner in self.partner:
            pl.semaphore_signal(
                barrier, inc=1, device_id={"fsdp": partner}, device_id_type=MESH
            )
        for rep in self.other_rep:
            pl.semaphore_signal(barrier, inc=1, device_id={"rep": rep}, device_id_type=MESH)
        pl.semaphore_wait(barrier, self.bits + self.reps - 1)

    def base(self, k):
        return self.slot // (1 << k) * (1 << k)

    def partner_base(self, k):
        return self.base(k) + (1 << k) * (1 - 2 * self.bit[self.bits - 1 - k])


class Gather:
    def __init__(self, place, out, fs, fr, xs, xr, ws, wr):
        self.place, self.out = place, out
        self.fs, self.fr, self.xs, self.xr, self.ws, self.wr = fs, fr, xs, xr, ws, wr
        self.sent = []

    def _send(self, src, dst, send, recv, device):
        copy = pltpu.make_async_remote_copy(
            src_ref=src, dst_ref=dst, send_sem=send, recv_sem=recv,
            device_id=device, device_id_type=MESH,
        )
        copy.start()
        self.sent.append(copy)

    def across(self, piece, src, first, count):
        reps = self.place.reps
        for d in range(1, reps):
            self._send(
                src, self.out.at[reps - d, pl.ds(first, count)],
                self.xs.at[d - 1, piece], self.xr.at[reps - d - 1, piece],
                {"rep": self.place.other_rep[d - 1]},
            )

    def stage(self, k, src=None):
        place = self.place
        window = self.out.at[0, pl.ds(place.base(k), 1 << k)]
        self._send(
            window if src is None else src, window, self.fs.at[k], self.fr.at[k],
            {"fsdp": place.partner[place.bits - 1 - k]},
        )

    def start(self, src):
        self.stage(0, src)
        self.across(0, src, self.place.slot, 1)

    def arrive(self, k):
        window = self.out.at[0, pl.ds(self.place.partner_base(k), 1 << k)]
        pltpu.make_async_copy(window, window, self.fr.at[k]).wait()

    def forward(self, k):
        place = self.place
        self.arrive(k)
        if k + 1 < place.bits:
            self.stage(k + 1)
            first = place.partner_base(k)
            self.across(k + 1, self.out.at[0, pl.ds(first, 1 << k)], first, 1 << k)

    def pieces(self):
        yield 0, self.place.slot, 1
        for k in range(self.place.bits - 1):
            yield k + 1, self.place.partner_base(k), 1 << k

    def relay(self, piece, first, count):
        for d in range(1, self.place.reps):
            window = self.out.at[d, pl.ds(first, count)]
            pltpu.make_async_copy(window, window, self.xr.at[d - 1, piece]).wait()
            self._send(
                window, window, self.ws.at[d - 1, piece], self.wr.at[d - 1, piece],
                {"fsdp": self.place.partner[0]},
            )

    def finish(self):
        place = self.place
        for piece, first, count in self.pieces():
            far = first + place.partner_base(place.bits - 1) - place.base(place.bits - 1)
            for d in range(1, place.reps):
                window = self.out.at[d, pl.ds(far, count)]
                pltpu.make_async_copy(window, window, self.wr.at[d - 1, piece]).wait()
        for copy in self.sent:
            copy.wait_send()


def gather_semaphores(reps, bits):
    dma = pltpu.SemaphoreType.DMA
    others = max(reps - 1, 1)
    return [dma((bits,)), dma((bits,))] + [dma((others, bits))] * 4


def tokens_kernel(reps, bits, tokens_ref, out_ref, local, *sems):
    place = Place(reps, bits)
    own = pltpu.make_async_copy(tokens_ref, out_ref.at[0, pl.ds(place.slot, 1)], local)
    own.start()
    place.meet()
    gather = Gather(place, out_ref, *sems)
    gather.start(tokens_ref)
    own.wait()
    for k in range(bits - 1):
        gather.forward(k)
    for piece in gather.pieces():
        gather.relay(*piece)
    gather.arrive(bits - 1)
    gather.finish()


def errors_kernel(reps, bits, *refs):
    primal_ref, tangent_ref, targets_ref, error_ref, error_tangent_ref = refs[:5]
    refs = refs[5:]
    parts = (primal_ref, tangent_ref)
    outs = (error_ref, error_tangent_ref)
    landing = [refs[c * bits : (c + 1) * bits] for c in range(2)]
    refs = refs[2 * bits :]
    totals = [refs[c * bits : (c + 1) * bits] for c in range(2)]
    refs = refs[2 * bits :]
    send, recv, local = refs[:3]
    sems = [refs[3:9], refs[9:15]]

    place = Place(reps, bits)
    place.meet()
    copies = {}

    def begin(c, j, src):
        half = 1 << (bits - 1 - j)
        copies[c, j] = pltpu.make_async_remote_copy(
            src_ref=src.at[pl.ds((1 - place.bit[j]) * half, half)],
            dst_ref=landing[c][j],
            send_sem=send.at[c, j],
            recv_sem=recv.at[c, j],
            device_id={"fsdp": place.partner[j]},
            device_id_type=MESH,
        )
        copies[c, j].start()

    current = list(parts)
    for c in range(2):
        begin(c, 0, current[c])
    gathers = [Gather(place, outs[c], *sems[c]) for c in range(2)]
    own = []
    for j in range(bits):
        half = 1 << (bits - 1 - j)
        for c in range(2):
            copies[c, j].wait_recv()
            keep = place.bit[j] * half
            source, came, total = current[c], landing[c][j], totals[c][j]
            if j < bits - 1:

                def add(i, carry, source=source, came=came, total=total, keep=keep):
                    total[i] = (source[keep + i].astype(F32) + came[i].astype(F32)).astype(BF16)
                    return carry

                lax.fori_loop(0, half, add, 0)
                current[c] = total
                begin(c, j + 1, total)
            else:
                whole = source[keep].astype(F32) + came[0].astype(F32)
                if c == 0:
                    whole = whole - targets_ref[0].astype(F32)
                total[0] = whole.astype(BF16)
                gathers[c].start(total)
                own.append(
                    pltpu.make_async_copy(
                        total, outs[c].at[0, pl.ds(place.slot, 1)], local.at[c]
                    )
                )
                own[c].start()
    for c in range(2):
        own[c].wait()
    for k in range(bits - 1):
        for c in range(2):
            gathers[c].forward(k)
    for k, piece in enumerate(gathers[0].pieces()):
        for c in range(2):
            gathers[c].relay(*piece)
    for c in range(2):
        gathers[c].arrive(bits - 1)
        gathers[c].finish()
    for copy in copies.values():
        copy.wait_send()


def vmem(count):
    return [pl.BlockSpec(memory_space=pltpu.VMEM)] * count


def gather_tokens(tokens, reps, bits):
    rows, width = tokens.shape
    fsdp = 1 << bits
    out = pl.pallas_call(
        functools.partial(tokens_kernel, reps, bits),
        out_shape=jax.ShapeDtypeStruct((reps, fsdp, rows, width), BF16),
        in_specs=vmem(1),
        out_specs=vmem(1)[0],
        scratch_shapes=[pltpu.SemaphoreType.DMA] + gather_semaphores(reps, bits),
        compiler_params=pltpu.CompilerParams(collective_id=0, has_side_effects=True),
        cost_estimate=pl.CostEstimate(flops=0, bytes_accessed=60_000_000, transcendentals=0),
        name="tokens_gather",
    )(tokens.reshape(1, rows, width))
    return out.reshape(reps * fsdp * rows, width)


def exchange_errors(primal, tangent, targets, reps, bits):
    rows, width = targets.shape
    fsdp = 1 << bits
    dma = pltpu.SemaphoreType.DMA
    halves = [pltpu.VMEM((1 << (bits - 1 - j), rows, width), BF16) for j in range(bits)]
    shape = jax.ShapeDtypeStruct((reps, fsdp, rows, width), BF16)
    error, error_tangent = pl.pallas_call(
        functools.partial(errors_kernel, reps, bits),
        out_shape=(shape, shape),
        in_specs=vmem(3),
        out_specs=tuple(vmem(2)),
        scratch_shapes=halves * 4
        + [dma((2, bits)), dma((2, bits)), dma((2,))]
        + gather_semaphores(reps, bits) * 2,
        compiler_params=pltpu.CompilerParams(
            collective_id=1, has_side_effects=True, vmem_limit_bytes=56 * 1024 * 1024
        ),
        cost_estimate=pl.CostEstimate(flops=0, bytes_accessed=120_000_000, transcendentals=0),
        name="errors_exchange",
    )(
        primal.reshape(fsdp, rows, width),
        tangent.reshape(fsdp, rows, width),
        targets.reshape(1, rows, width),
    )
    total = reps * fsdp * rows
    return error.reshape(total, width), error_tangent.reshape(total, width)


def on_device(
    reps,
    bits,
    tokens,
    targets,
    gate_weight,
    up_weight,
    down_weight,
    gate_direction,
    up_direction,
    down_direction,
):
    gathered = gather_tokens(tokens, reps, bits)
    mine = gathered.shape[0] // reps
    gate = jnp.dot(gathered, gate_weight, preferred_element_type=F32)
    up = jnp.dot(gathered, up_weight, preferred_element_type=F32)
    gate_tangent = jnp.dot(gathered, gate_direction, preferred_element_type=F32)
    up_tangent = jnp.dot(gathered, up_direction, preferred_element_type=F32)
    activation, slope, bend = silu_parts(gate)
    hidden = (activation * up).astype(BF16)
    hidden_tangent = (slope * gate_tangent * up + activation * up_tangent).astype(BF16)
    primal = jnp.dot(hidden[:mine], down_weight, preferred_element_type=F32).astype(BF16)
    tangent = (
        jnp.dot(hidden_tangent[:mine], down_weight, preferred_element_type=F32)
        + jnp.dot(hidden[:mine], down_direction, preferred_element_type=F32)
    ).astype(BF16)
    error, error_tangent = exchange_errors(primal, tangent, targets, reps, bits)
    back = jnp.dot(error, down_weight.T, preferred_element_type=F32)
    back_tangent = jnp.dot(error_tangent, down_weight.T, preferred_element_type=F32) + jnp.dot(
        error, down_direction.T, preferred_element_type=F32
    )
    gate_grad_tangent = (
        back_tangent * up * slope + back * up_tangent * slope + back * up * bend * gate_tangent
    ).astype(BF16)
    up_grad_tangent = (back_tangent * activation + back * slope * gate_tangent).astype(BF16)
    hvp_gate = inner_rows(gathered, gate_grad_tangent)
    hvp_up = inner_rows(gathered, up_grad_tangent)
    hvp_down = inner_rows(
        jnp.concatenate([hidden_tangent, hidden], axis=0),
        jnp.concatenate([error, error_tangent], axis=0),
    )
    return (hvp_gate, hvp_up, hvp_down)


def solution(mesh):
    reps = mesh.shape["rep"]
    bits = mesh.shape["fsdp"].bit_length() - 1
    in_specs = (
        P(("rep", "fsdp"), None),
        P(("rep", "fsdp"), None),
        P(None, "fsdp"),
        P(None, "fsdp"),
        P("fsdp", None),
        P(None, "fsdp"),
        P(None, "fsdp"),
        P("fsdp", None),
    )
    out_specs = (P(None, "fsdp"), P(None, "fsdp"), P("fsdp", None))
    return jax.shard_map(
        functools.partial(on_device, reps, bits),
        mesh=mesh, in_specs=in_specs, out_specs=out_specs, check_vma=False,
    )
```

time: 296 us -> 142 us (0.48)
  blocking collectives: 127 us -> 0 us
  Pallas kernels: 0 us -> 78.5 us
  waiting for transfers between devices: 65.9 us -> 0 us
  matrix products: 81.6 us -> 58.5 us
  between operations: 15.9 us -> 0.92 us
  other arithmetic: 3 us -> 0.01 us
    all_gather x7 -> x0, blocking collectives: 127 us -> none  [the longest x1 26.1 us: on_device(): gathered = lax.all_gather(tokens, 'fsdp', axis=0, tiled=True)]
    pallas_call x0 -> x2, Pallas kernels: none -> 78.5 us  [the longest x1 52.6 us: exchange_errors(): pl.pallas_call(functools.partial(errors_kernel, reps, bits), out_shape=(s...]
    reduce_scatter x1 -> x0, waiting for transfers between devices: 65.3 us -> none  [on_device(): lax.psum_scatter(jnp.concatenate([primal, tangent], axis=1), 'fsdp', scat...]
    dot_general x4 -> x3, matrix products: 43.9 us -> 27 us  [inner_rows(): lax.dot_general(left, right, (((0,), (0,)), ((), ())), preferred_element_...]
    dot_general x10, matrix products: 37.6 us -> 31.6 us  [the longest x1 6.54 us: on_device(): back = jnp.dot(error, down_weight.T, preferred_element_type=F32)]
  transfers between devices with their start and end apart: 4 -> 0, of which waited for: 1 -> 0; matrix products, arithmetic and copies ran while one was open for 17% -> 0% of each run, Pallas kernels for 0% -> 0%
where the time goes in v1:
time: 142 us; the launch traced here: 140 us
  Pallas kernels  78.5 us (55%)
  matrix products  58.5 us (41%)
  local copies, waits for them, and re-layouts  1.95 us (1%)
    pallas_call x1, Pallas kernels, exchange_errors(): pl.pallas_call(functools.partial(errors_kernel, reps, bits), out_shape=(s...  52.6 us
    dot_general x3, matrix products, inner_rows(): lax.dot_general(left, right, (((0,), (0,)), ((), ())), preferred_element_...  27 us
    pallas_call x1, Pallas kernels, gather_tokens(): pl.pallas_call(functools.partial(tokens_kernel, reps, bits), out_shape=ja...  25.8 us
    dot_general x1, matrix products, on_device(): back = jnp.dot(error, down_weight.T, preferred_element_type=F32)  6.54 us
    dot_general x1, matrix products, on_device(): gate_tangent = jnp.dot(gathered, gate_direction, preferred_element_type=F32)  6.51 us
    dot_general x1, matrix products, on_device(): up_tangent = jnp.dot(gathered, up_direction, preferred_element_type=F32)  2.84 us

profile of v1, /device:TPU:0, one launch (start us, length us, event | category | flops | bytes accessed | tf_op | source)
XLA Modules:
  0.0 139.9 jit_solution(6808200971030040493)
XLA Ops:
  0.6 25.8 %tokens_gather.1 = bf16[2,16,8,3584]{3,2,1,0:T(8,128)(2,1)} custom-call(bf16[1,8,3584]{2,1,0:T(8,128)(2,1)} %bitcast.46), custom_call_target="tpu_custom_call" | custom-call | bytes 60000000 | tf_op jit(solution)/shard_map/tokens_gather/pallas_call | solution.py:229
  26.4 0.0 copy-start
  26.5 0.0 copy-start.1
  26.5 0.0 slice-start.12
  26.5 0.0 slice-start.13
  26.5 6.5 %fusion.33 = f32[256,1184]{0,1:T(8,128)S(1)} fusion(bf16[256,3584]{1,0:T(8,128)(2,1)} %bitcast.40, bf16[3584,1184]{0,1:T(8,128)(2,1)} %param.13), kind=kOutput, calls=%fused_computation.40 | convolution fusion | flops 2172649472 | bytes 11534336 | tf_op jit(solution)/shard_map/dot_general | solution.py:286
  33.0 0.0 copy-done
  33.0 0.4 copy-done.1
  33.4 0.0 slice-start.14
  33.4 0.0 slice-start.15
  33.4 0.0 slice-start.16
  33.4 2.4 %fusion.31 = f32[256,1184]{0,1:T(8,128)S(1)} fusion(bf16[256,3584]{1,0:T(8,128)(2,1)S(1)} %bitcast.41, bf16[3584,1184]{0,1:T(8,128)(2,1)S(1)} %copy-done.1), kind=kOutput, calls=%fused_computation.38 | convolution fusion | flops 2172649472 | bytes 11534336 | tf_op jit(solution)/shard_map/dot_general | solution.py:284
  35.8 0.0 slice-done.12
  35.8 0.0 slice-done.13
  35.8 0.1 slice-done.14
  35.9 0.0 slice-start.17
  35.9 0.0 slice-start
  35.9 0.0 slice-start.1
  35.9 2.4 %fusion.32 = f32[256,1184]{0,1:T(8,128)S(1)} fusion(bf16[256,3584]{1,0:T(8,128)(2,1)S(1)} %bitcast.42, bf16[3584,1184]{0,1:T(8,128)(2,1)S(1)} %bitcast.49), kind=kOutput, calls=%fused_computation.39 | convolution fusion | flops 2172649472 | bytes 11534336 | tf_op jit(solution)/shard_map/dot_general | solution.py:285
  38.3 0.0 slice-done.15
  38.3 0.1 slice-done.16
  38.4 0.0 slice-done.17
  38.4 0.0 slice-start.2
  38.4 2.8 %add_convert_fusion.1 = (bf16[256,1184]{0,1:T(8,128)(2,1)S(1)}, bf16[256,1184]{0,1:T(8,128)(2,1)S(1)}, f32[256,1184]{0,1:T(8,128)S(1)}) fusion(f32[256,1184]{0,1:T(8,128)S(1)} %fusion.32, f32[256,1184]{0,1:T(8,128)S(1)} %fusion.33, f32[256,1184]{0,1:T(8,128)S(1)} %fusion.31, bf16[256,3584]{1,0:T(8,128)(2,1)S(1)} %bitcast.43, bf16[3584,1184]{0,1:T(8,128)(2,1)S(1)} %bitcast.51), kind=kOutput, calls=%fused_computation.25 | convolution fusion | flops 2177196032 | bytes 16384000 | tf_op jit(solution)/shard_map/dot_general | solution.py:287
  41.3 0.0 slice-done
  41.3 0.0 slice-done.1
  41.3 0.0 slice-done.2
  41.3 0.0 slice-start.6
  41.3 0.0 slice-start.7
  41.3 2.3 %fusion.1.refs_0_ = bf16[16,8,3584]{2,1,0:T(8,128)(2,1)} fusion(bf16[1184,3584]{1,0:T(8,128)(2,1)S(1)} %bitcast.33, bf16[256,1184]{0,1:T(8,128)(2,1)S(1)} %get-tuple-element.8), kind=kOutput, calls=%fused_computation.5 | convolution fusion | flops 1086783488 | bytes 9707520 | tf_op jit(solution)/shard_map/dot_general | solution.py:291
  43.6 0.0 slice-start.8
  43.6 1.4 fusion.21
  45.0 0.0 slice-done.6
  45.0 0.1 slice-done.7
  45.1 0.0 slice-done.8
  45.1 2.3 %fusion.2.refs_1_ = bf16[16,8,3584]{2,1,0:T(8,128)(2,1)} fusion(f32[128,3584]{1,0:T(8,128)S(1)} %fusion.21, bf16[1184,3584]{1,0:T(8,128)(2,1)S(1)} %bitcast.37, bf16[256,1184]{0,1:T(8,128)(2,1)S(1)} %get-tuple-element.8), kind=kOutput, calls=%fused_computation.6 | convolution fusion | flops 1087242240 | bytes 11542528 | tf_op jit(solution)/shard_map/dot_general | solution.py:294
  47.4 0.0 slice-start.3
  47.4 52.6 %errors_exchange.1 = (bf16[2,16,8,3584]{3,2,1,0:T(8,128)(2,1)}, bf16[2,16,8,3584]{3,2,1,0:T(8,128)(2,1)}) custom-call(bf16[16,8,3584]{2,1,0:T(8,128)(2,1)} %fusion.1.refs_0_, bf16[16,8,3584]{2,1,0:T(8,128)(2,1)} %fusion.2.refs_1_, bf16[1,8,3584]{2,1,0:T(8,128)(2,1)} %bitcast.47), custom_call_target="tpu_custom_call" | custom-call | bytes 120000000 | tf_op jit(solution)/shard_map/errors_exchange/pallas_call | solution.py:248
  100.1 0.0 slice-start.4
  100.1 0.0 slice-start.5
  100.1 0.0 copy-start.3
  100.1 0.0 slice-start.9
  100.2 0.0 slice-start.10
  100.2 6.5 %fusion.35 = f32[256,1184]{0,1:T(8,128)S(1)} fusion(bf16[256,3584]{1,0:T(8,128)(2,1)} %bitcast.52, bf16[1184,3584]{1,0:T(8,128)(2,1)} %param.12), kind=kOutput, calls=%fused_computation.42 | convolution fusion | flops 2172649472 | bytes 11534336 | tf_op jit(solution)/shard_map/dot_general | solution.py:297
  106.7 0.0 slice-done.3
  106.7 0.0 slice-done.4
  106.7 0.0 slice-done.5
  106.7 0.3 copy-done.3
  107.1 0.0 slice-start.11
  107.1 0.0 copy-start.2
  107.1 2.4 %fusion.34 = f32[256,1184]{0,1:T(8,128)S(1)} fusion(bf16[256,3584]{1,0:T(8,128)(2,1)S(1)} %bitcast.55, bf16[1184,3584]{1,0:T(8,128)(2,1)S(1)} %bitcast.35), kind=kOutput, calls=%fused_computation.41 | convolution fusion | flops 2172649472 | bytes 11534336 | tf_op jit(solution)/shard_map/dot_general | solution.py:298
  109.5 0.0 slice-done.9
  109.5 0.0 slice-done.10
  109.5 0.4 slice-done.11
  109.9 0.5 copy-done.2
  110.4 2.5 %convolution_add_fusion.1 = f32[256,1184]{0,1:T(8,128)S(1)} fusion(f32[256,1184]{0,1:T(8,128)S(1)} %fusion.34, bf16[256,3584]{1,0:T(8,128)(2,1)S(1)} %bitcast.53, bf16[1184,3584]{1,0:T(8,128)(2,1)S(1)} %bitcast.39), kind=kOutput, calls=%fused_computation.11 | convolution fusion | flops 2172952576 | bytes 12746752 | tf_op jit(solution)/shard_map/dot_general | solution.py:298
  112.9 9.2 %convolution_bitcast_fusion.1 = f32[3584,1184]{0,1:T(8,128)} fusion(bf16[256,3584]{1,0:T(8,128)(2,1)S(1)} %bitcast.44, f32[256,1184]{0,1:T(8,128)S(1)} %fusion.33, f32[256,1184]{0,1:T(8,128)S(1)} %fusion.31, f32[256,1184]{0,1:T(8,128)S(1)} %fusion.35, f32[256,1184]{0,1:T(8,128)S(1)} %fusion.32, f32[256,1184]{0,1:T(8,128)S(1)} %get-tuple-element.9, ...), kind=kOutput, calls=%fused_computation.1 | convolution fusion | flops 2179317760 | bytes 26083328 | tf_op jit(solution)/shard_map/dot_general | solution.py:23
  122.1 9.1 %convolution_bitcast_fusion = f32[3584,1184]{0,1:T(8,128)} fusion(bf16[256,3584]{1,0:T(8,128)(2,1)S(1)} %bitcast.45, f32[256,1184]{0,1:T(8,128)S(1)} %fusion.33, f32[256,1184]{0,1:T(8,128)S(1)} %fusion.35, f32[256,1184]{0,1:T(8,128)S(1)} %convolution_add_fusion.1, f32[256,1184]{0,1:T(8,128)S(1)} %fusion.31), kind=kOutput, calls=%fused_computation | convolution fusion | flops 2176589824 | bytes 23658496 | tf_op jit(solution)/shard_map/dot_general | solution.py:23
  131.3 8.6 %fusion.3 = f32[1184,3584]{1,0:T(8,128)} fusion(bf16[256,3584]{1,0:T(8,128)(2,1)S(1)} %bitcast.56, bf16[256,3584]{1,0:T(8,128)(2,1)S(1)} %bitcast.54, bf16[256,1184]{0,1:T(8,128)(2,1)S(1)} %get-tuple-element.8, bf16[256,1184]{0,1:T(8,128)(2,1)S(1)} %get-tuple-element.7), kind=kOutput, calls=%fused_computation.7 | convolution fusion | flops 4355063808 | bytes 21856256 | tf_op jit(solution)/shard_map/dot_general | solution.py:23
  (6 shorter events, 0.0 us)
Async XLA Ops:
  26.4 6.6 %copy-start = (bf16[2,16,8,3584]{3,2,1,0:T(8,128)(2,1)S(1)}, bf16[2,16,8,3584]{3,2,1,0:T(8,128)(2,1)}, u32[]{:S(2)}) copy-start(bf16[2,16,8,3584]{3,2,1,0:T(8,128)(2,1)} %tokens_gather.1) | copy-start | bytes 5505028
  26.5 6.9 %copy-start.1 = (bf16[3584,1184]{0,1:T(8,128)(2,1)S(1)}, bf16[3584,1184]{0,1:T(8,128)(2,1)}, u32[]{:S(2)}) copy-start(bf16[3584,1184]{0,1:T(8,128)(2,1)} %param.10) | copy-start | bytes 25460740
  26.5 9.3 %slice-start.12 = ((s8[8486912]{0:T(1024)(128)(4,1)}), s8[4194304]{0:T(1024)(128)(4,1)S(1)}, s32[]{:S(2)}) async-start(s8[8486912]{0:T(1024)(128)(4,1)} %bitcast.48), calls=%async_computation.12 | async-start | bytes 8388608
  26.5 9.3 %slice-start.13 = ((s8[8486912]{0:T(1024)(128)(4,1)}), s8[4194304]{0:T(1024)(128)(4,1)S(1)}, s32[]{:S(2)}) async-start(s8[8486912]{0:T(1024)(128)(4,1)} %bitcast.48), calls=%async_computation.13 | async-start | bytes 8388608
  33.4 2.5 %slice-start.14 = ((s8[8486912]{0:T(1024)(128)(4,1)}), s8[98304]{0:T(1024)(128)(4,1)S(1)}, s32[]{:S(2)}) async-start(s8[8486912]{0:T(1024)(128)(4,1)} %bitcast.48), calls=%async_computation.14 | async-start | bytes 196608
  33.4 4.9 %slice-start.15 = ((s8[8486912]{0:T(1024)(128)(4,1)}), s8[4194304]{0:T(1024)(128)(4,1)S(1)}, s32[]{:S(2)}) async-start(s8[8486912]{0:T(1024)(128)(4,1)} %bitcast.50), calls=%async_computation.15 | async-start | bytes 8388608
  33.4 5.0 %slice-start.16 = ((s8[8486912]{0:T(1024)(128)(4,1)}), s8[4194304]{0:T(1024)(128)(4,1)S(1)}, s32[]{:S(2)}) async-start(s8[8486912]{0:T(1024)(128)(4,1)} %bitcast.50), calls=%async_computation.16 | async-start | bytes 8388608
  35.9 2.5 %slice-start.17 = ((s8[8486912]{0:T(1024)(128)(4,1)}), s8[98304]{0:T(1024)(128)(4,1)S(1)}, s32[]{:S(2)}) async-start(s8[8486912]{0:T(1024)(128)(4,1)} %bitcast.50), calls=%async_computation.17 | async-start | bytes 196608
  35.9 5.4 %slice-start = ((s8[8486912]{0:T(1024)(128)(4,1)}), s8[4194304]{0:T(1024)(128)(4,1)S(1)}, s32[]{:S(2)}) async-start(s8[8486912]{0:T(1024)(128)(4,1)} %bitcast.32), calls=%async_computation | async-start | bytes 8388608
  35.9 5.4 %slice-start.1 = ((s8[8486912]{0:T(1024)(128)(4,1)}), s8[4194304]{0:T(1024)(128)(4,1)S(1)}, s32[]{:S(2)}) async-start(s8[8486912]{0:T(1024)(128)(4,1)} %bitcast.32), calls=%async_computation.1 | async-start | bytes 8388608
  38.4 2.9 %slice-start.2 = ((s8[8486912]{0:T(1024)(128)(4,1)}), s8[98304]{0:T(1024)(128)(4,1)S(1)}, s32[]{:S(2)}) async-start(s8[8486912]{0:T(1024)(128)(4,1)} %bitcast.32), calls=%async_computation.2 | async-start | bytes 196608
  41.3 3.7 %slice-start.6 = ((s8[8486912]{0:T(1024)(128)(4,1)}), s8[4194304]{0:T(1024)(128)(4,1)S(1)}, s32[]{:S(2)}) async-start(s8[8486912]{0:T(1024)(128)(4,1)} %bitcast.36), calls=%async_computation.6 | async-start | bytes 8388608
  41.3 3.8 %slice-start.7 = ((s8[8486912]{0:T(1024)(128)(4,1)}), s8[4194304]{0:T(1024)(128)(4,1)S(1)}, s32[]{:S(2)}) async-start(s8[8486912]{0:T(1024)(128)(4,1)} %bitcast.36), calls=%async_computation.7 | async-start | bytes 8388608
  43.6 1.5 %slice-start.8 = ((s8[8486912]{0:T(1024)(128)(4,1)}), s8[98304]{0:T(1024)(128)(4,1)S(1)}, s32[]{:S(2)}) async-start(s8[8486912]{0:T(1024)(128)(4,1)} %bitcast.36), calls=%async_computation.8 | async-start | bytes 196608
  47.4 59.3 %slice-start.3 = ((s8[8486912]{0:T(1024)(128)(4,1)}), s8[98304]{0:T(1024)(128)(4,1)S(1)}, s32[]{:S(2)}) async-start(s8[8486912]{0:T(1024)(128)(4,1)} %bitcast.34), calls=%async_computation.3 | async-start | bytes 196608
  100.1 6.6 %slice-start.4 = ((s8[8486912]{0:T(1024)(128)(4,1)}), s8[4194304]{0:T(1024)(128)(4,1)S(1)}, s32[]{:S(2)}) async-start(s8[8486912]{0:T(1024)(128)(4,1)} %bitcast.34), calls=%async_computation.4 | async-start | bytes 8388608
  100.1 6.6 %slice-start.5 = ((s8[8486912]{0:T(1024)(128)(4,1)}), s8[4194304]{0:T(1024)(128)(4,1)S(1)}, s32[]{:S(2)}) async-start(s8[8486912]{0:T(1024)(128)(4,1)} %bitcast.34), calls=%async_computation.5 | async-start | bytes 8388608
  100.1 6.9 %copy-start.3 = (bf16[2,16,8,3584]{3,2,1,0:T(8,128)(2,1)S(1)}, bf16[2,16,8,3584]{3,2,1,0:T(8,128)(2,1)}, u32[]{:S(2)}) copy-start(bf16[2,16,8,3584]{3,2,1,0:T(8,128)(2,1)} %get-tuple-element.5) | copy-start | bytes 5505028
  100.1 9.3 %slice-start.9 = ((s8[8486912]{0:T(1024)(128)(4,1)}), s8[4194304]{0:T(1024)(128)(4,1)S(1)}, s32[]{:S(2)}) async-start(s8[8486912]{0:T(1024)(128)(4,1)} %bitcast.38), calls=%async_computation.9 | async-start | bytes 8388608
  100.2 9.3 %slice-start.10 = ((s8[8486912]{0:T(1024)(128)(4,1)}), s8[4194304]{0:T(1024)(128)(4,1)S(1)}, s32[]{:S(2)}) async-start(s8[8486912]{0:T(1024)(128)(4,1)} %bitcast.38), calls=%async_computation.10 | async-start | bytes 8388608
  107.1 2.8 %slice-start.11 = ((s8[8486912]{0:T(1024)(128)(4,1)}), s8[98304]{0:T(1024)(128)(4,1)S(1)}, s32[]{:S(2)}) async-start(s8[8486912]{0:T(1024)(128)(4,1)} %bitcast.38), calls=%async_computation.11 | async-start | bytes 196608
  107.1 3.4 %copy-start.2 = (bf16[2,16,8,3584]{3,2,1,0:T(8,128)(2,1)S(1)}, bf16[2,16,8,3584]{3,2,1,0:T(8,128)(2,1)}, u32[]{:S(2)}) copy-start(bf16[2,16,8,3584]{3,2,1,0:T(8,128)(2,1)} %get-tuple-element.6) | copy-start | bytes 5505028

commit v2 on v1

--- a/solution.py
+++ b/solution.py
@@ -8,6 +8,7 @@
 from jax.sharding import PartitionSpec as P
 
 MESH = pl.DeviceIdType.MESH
+SPLIT = 2
 F32 = jnp.float32
 BF16 = jnp.bfloat16
 
@@ -147,14 +148,17 @@
 def errors_kernel(reps, bits, *refs):
     primal_ref, tangent_ref, targets_ref, error_ref, error_tangent_ref = refs[:5]
     refs = refs[5:]
-    parts = (primal_ref, tangent_ref)
-    outs = (error_ref, error_tangent_ref)
-    landing = [refs[c * bits : (c + 1) * bits] for c in range(2)]
-    refs = refs[2 * bits :]
-    totals = [refs[c * bits : (c + 1) * bits] for c in range(2)]
-    refs = refs[2 * bits :]
+    width = targets_ref.shape[2] // SPLIT
+    spans = [(part, pl.ds(i * width, width)) for part in range(2) for i in range(SPLIT)]
+    parts = [(primal_ref, tangent_ref)[part].at[:, :, span] for part, span in spans]
+    outs = [(error_ref, error_tangent_ref)[part].at[:, :, :, span] for part, span in spans]
+    chunks = range(len(spans))
+    landing = [refs[c * bits : (c + 1) * bits] for c in chunks]
+    refs = refs[len(spans) * bits :]
+    totals = [refs[c * bits : (c + 1) * bits] for c in chunks]
+    refs = refs[len(spans) * bits :]
     send, recv, local = refs[:3]
-    sems = [refs[3:9], refs[9:15]]
+    sems = [refs[3 + 6 * c : 9 + 6 * c] for c in chunks]
 
     place = Place(reps, bits)
     place.meet()
@@ -173,13 +177,13 @@
         copies[c, j].start()
 
     current = list(parts)
-    for c in range(2):
+    for c in chunks:
         begin(c, 0, current[c])
-    gathers = [Gather(place, outs[c], *sems[c]) for c in range(2)]
+    gathers = [Gather(place, outs[c], *sems[c]) for c in chunks]
     own = []
     for j in range(bits):
         half = 1 << (bits - 1 - j)
-        for c in range(2):
+        for c in chunks:
             copies[c, j].wait_recv()
             keep = place.bit[j] * half
             source, came, total = current[c], landing[c][j], totals[c][j]
@@ -194,8 +198,8 @@
                 begin(c, j + 1, total)
             else:
                 whole = source[keep].astype(F32) + came[0].astype(F32)
-                if c == 0:
-                    whole = whole - targets_ref[0].astype(F32)
+                if spans[c][0] == 0:
+                    whole = whole - targets_ref[0, :, spans[c][1]].astype(F32)
                 total[0] = whole.astype(BF16)
                 gathers[c].start(total)
                 own.append(
@@ -204,15 +208,15 @@
                     )
                 )
                 own[c].start()
-    for c in range(2):
+    for c in chunks:
         own[c].wait()
     for k in range(bits - 1):
-        for c in range(2):
+        for c in chunks:
             gathers[c].forward(k)
     for k, piece in enumerate(gathers[0].pieces()):
-        for c in range(2):
+        for c in chunks:
             gathers[c].relay(*piece)
-    for c in range(2):
+    for c in chunks:
         gathers[c].arrive(bits - 1)
         gathers[c].finish()
     for copy in copies.values():
@@ -232,7 +236,11 @@
         in_specs=vmem(1),
         out_specs=vmem(1)[0],
         scratch_shapes=[pltpu.SemaphoreType.DMA] + gather_semaphores(reps, bits),
-        compiler_params=pltpu.CompilerParams(collective_id=0, has_side_effects=True),
+        compiler_params=pltpu.CompilerParams(
+            collective_id=0,
+            has_side_effects=True,
+            vmem_limit_bytes=(reps * fsdp + 1) * rows * width * 2 + (2 << 20),
+        ),
         cost_estimate=pl.CostEstimate(flops=0, bytes_accessed=60_000_000, transcendentals=0),
         name="tokens_gather",
     )(tokens.reshape(1, rows, width))
@@ -243,18 +251,21 @@
     rows, width = targets.shape
     fsdp = 1 << bits
     dma = pltpu.SemaphoreType.DMA
-    halves = [pltpu.VMEM((1 << (bits - 1 - j), rows, width), BF16) for j in range(bits)]
+    halves = [pltpu.VMEM((1 << (bits - 1 - j), rows, width // SPLIT), BF16) for j in range(bits)]
+    chunks = 2 * SPLIT
+    block = rows * width * 2
+    limit = block * (2 * fsdp + 4 * fsdp + 2 * reps * fsdp + 2) + (2 << 20)
     shape = jax.ShapeDtypeStruct((reps, fsdp, rows, width), BF16)
     error, error_tangent = pl.pallas_call(
         functools.partial(errors_kernel, reps, bits),
         out_shape=(shape, shape),
         in_specs=vmem(3),
         out_specs=tuple(vmem(2)),
-        scratch_shapes=halves * 4
-        + [dma((2, bits)), dma((2, bits)), dma((2,))]
-        + gather_semaphores(reps, bits) * 2,
+        scratch_shapes=halves * (2 * chunks)
+        + [dma((chunks, bits)), dma((chunks, bits)), dma((chunks,))]
+        + gather_semaphores(reps, bits) * chunks,
         compiler_params=pltpu.CompilerParams(
-            collective_id=1, has_side_effects=True, vmem_limit_bytes=56 * 1024 * 1024
+            collective_id=1, has_side_effects=True, vmem_limit_bytes=limit
         ),
         cost_estimate=pl.CostEstimate(flops=0, bytes_accessed=120_000_000, transcendentals=0),
         name="errors_exchange",

time: 142 us -> 128 us (0.901); the launches traced: 140 us -> 128 us
  Pallas kernels: 78.5 us -> 70.2 us
  matrix products: 58.5 us -> 55.3 us
    pallas_call x1, Pallas kernels: 52.6 us -> 46.5 us  [exchange_errors(): pl.pallas_call(functools.partial(errors_kernel, reps, bits), out_shape=(s...]
    dot_general x1, matrix products: 6.54 us -> 2.4 us  [on_device(): back = jnp.dot(error, down_weight.T, preferred_element_type=F32)]
    dot_general x1, matrix products: 2.84 us -> 6.27 us  [on_device(): up_tangent = jnp.dot(gathered, up_direction, preferred_element_type=F32)]
    pallas_call x1, Pallas kernels: 25.8 us -> 23.7 us  [gather_tokens(): pl.pallas_call(functools.partial(tokens_kernel, reps, bits), out_shape=ja...]
where the time goes in v2:
time: 128 us
  Pallas kernels  70.2 us (55%)
  matrix products  55.3 us (43%)
  local copies, waits for them, and re-layouts  1.61 us (1%)
    pallas_call x1, Pallas kernels, exchange_errors(): pl.pallas_call(functools.partial(errors_kernel, reps, bits), out_shape=(s...  46.5 us
    dot_general x3, matrix products, inner_rows(): lax.dot_general(left, right, (((0,), (0,)), ((), ())), preferred_element_...  26.9 us
    pallas_call x1, Pallas kernels, gather_tokens(): pl.pallas_call(functools.partial(tokens_kernel, reps, bits), out_shape=ja...  23.7 us
    dot_general x1, matrix products, on_device(): up_tangent = jnp.dot(gathered, up_direction, preferred_element_type=F32)  6.27 us
    dot_general x1, matrix products, on_device(): gate_tangent = jnp.dot(gathered, gate_direction, preferred_element_type=F32)  5.95 us

profile of v2, /device:TPU:0, one launch (start us, length us, event | category | flops | bytes accessed | tf_op | source)
XLA Modules:
  0.0 128.0 jit_solution(9320792433378519304)
XLA Ops:
  0.6 0.0 copy-start
  0.6 0.8 copy-done
  1.4 0.0 slice-start.6
  1.5 23.7 %tokens_gather.1 = bf16[2,16,8,3584]{3,2,1,0:T(8,128)(2,1)S(1)} custom-call(bf16[1,8,3584]{2,1,0:T(8,128)(2,1)S(1)} %bitcast.38), custom_call_target="tpu_custom_call" | custom-call | bytes 60000000 | tf_op jit(solution)/shard_map/tokens_gather/pallas_call | solution.py:233
  25.2 0.0 slice-start.7
  25.2 0.0 slice-start.8
  25.2 0.0 slice-start.9
  25.2 0.0 slice-start.10
  25.2 6.0 %fusion.33 = f32[256,1184]{0,1:T(8,128)S(1)} fusion(bf16[256,3584]{1,0:T(8,128)(2,1)S(1)} %bitcast.32, bf16[3584,1184]{0,1:T(8,128)(2,1)} %param.13), kind=kOutput, calls=%fused_computation.40 | convolution fusion | flops 2172649472 | bytes 11534336 | tf_op jit(solution)/shard_map/dot_general | solution.py:297
  31.2 0.0 slice-done.6
  31.2 0.0 slice-done.7
  31.2 0.0 slice-done.8
  31.2 0.0 slice-start.11
  31.2 2.4 %fusion.31 = f32[256,1184]{0,1:T(8,128)S(1)} fusion(bf16[256,3584]{1,0:T(8,128)(2,1)S(1)} %bitcast.33, bf16[3584,1184]{0,1:T(8,128)(2,1)S(1)} %bitcast.50), kind=kOutput, calls=%fused_computation.38 | convolution fusion | flops 2172649472 | bytes 11534336 | tf_op jit(solution)/shard_map/dot_general | solution.py:295
  33.7 0.0 slice-done.9
  33.7 0.0 slice-done.10
  33.7 0.0 slice-done.11
  33.7 0.0 slice-start
  33.7 0.0 slice-start.1
  33.7 2.4 %fusion.32 = f32[256,1184]{0,1:T(8,128)S(1)} fusion(bf16[256,3584]{1,0:T(8,128)(2,1)S(1)} %bitcast.34, bf16[3584,1184]{0,1:T(8,128)(2,1)S(1)} %bitcast.52), kind=kOutput, calls=%fused_computation.39 | convolution fusion | flops 2172649472 | bytes 11534336 | tf_op jit(solution)/shard_map/dot_general | solution.py:296
  36.1 0.0 slice-start.2
  36.2 6.3 %add_convert_fusion.1 = (bf16[256,1184]{0,1:T(8,128)(2,1)S(1)}, bf16[256,1184]{0,1:T(8,128)(2,1)S(1)}, f32[256,1184]{0,1:T(8,128)S(1)}) fusion(f32[256,1184]{0,1:T(8,128)S(1)} %fusion.32, f32[256,1184]{0,1:T(8,128)S(1)} %fusion.33, f32[256,1184]{0,1:T(8,128)S(1)} %fusion.31, bf16[256,3584]{1,0:T(8,128)(2,1)S(1)} %bitcast.35, bf16[3584,1184]{0,1:T(8,128)(2,1)} %param.14), kind=kOutput, calls=%fused_computation.25 | convolution fusion | flops 2177196032 | bytes 16384000 | tf_op jit(solution)/shard_map/dot_general | solution.py:298
  42.4 0.0 slice-done
  42.4 0.0 slice-done.1
  42.4 0.0 slice-done.2
  42.5 0.0 slice-start.3
  42.5 0.0 slice-start.4
  42.5 1.4 %fusion.1.refs_0_ = bf16[16,8,3584]{2,1,0:T(8,128)(2,1)S(1)} fusion(bf16[1184,3584]{1,0:T(8,128)(2,1)S(1)} %bitcast.46, bf16[256,1184]{0,1:T(8,128)(2,1)S(1)} %get-tuple-element.8), kind=kOutput, calls=%fused_computation.5 | convolution fusion | flops 1086783488 | bytes 9707520 | tf_op jit(solution)/shard_map/dot_general | solution.py:302
  43.9 0.0 slice-start.5
  43.9 1.4 %fusion.21 = f32[128,3584]{1,0:T(8,128)S(1)} fusion(bf16[1184,3584]{1,0:T(8,128)(2,1)S(1)} %bitcast.46, bf16[256,1184]{0,1:T(8,128)(2,1)S(1)} %get-tuple-element.7), kind=kOutput, calls=%fused_computation.31 | convolution fusion | flops 1086324736 | bytes 10625024 | tf_op jit(solution)/shard_map/dot_general | solution.py:304
  45.3 0.0 slice-done.3
  45.3 0.7 slice-done.4
  45.9 0.1 slice-done.5
  46.0 0.0 copy-start.1
  46.0 1.4 %fusion.2.refs_1_ = bf16[16,8,3584]{2,1,0:T(8,128)(2,1)S(1)} fusion(f32[128,3584]{1,0:T(8,128)S(1)} %fusion.21, bf16[1184,3584]{1,0:T(8,128)(2,1)S(1)} %bitcast.48, bf16[256,1184]{0,1:T(8,128)(2,1)S(1)} %get-tuple-element.8), kind=kOutput, calls=%fused_computation.6 | convolution fusion | flops 1087242240 | bytes 11542528 | tf_op jit(solution)/shard_map/dot_general | solution.py:305
  47.4 0.0 copy-done.1
  47.4 46.5 %errors_exchange.1 = (bf16[2,16,8,3584]{3,2,1,0:T(8,128)(2,1)S(1)}, bf16[2,16,8,3584]{3,2,1,0:T(8,128)(2,1)S(1)}) custom-call(bf16[16,8,3584]{2,1,0:T(8,128)(2,1)S(1)} %fusion.1.refs_0_, bf16[16,8,3584]{2,1,0:T(8,128)(2,1)S(1)} %fusion.2.refs_1_, bf16[1,8,3584]{2,1,0:T(8,128)(2,1)S(1)} %bitcast.39), custom_call_target="tpu_custom_call" | custom-call | bytes 120000000 | tf_op jit(solution)/shard_map/errors_exchange/pallas_call | solution.py:259
  93.9 2.4 %fusion.35 = f32[256,1184]{0,1:T(8,128)S(1)} fusion(bf16[256,3584]{1,0:T(8,128)(2,1)S(1)} %bitcast.40, bf16[1184,3584]{1,0:T(8,128)(2,1)S(1)} %bitcast.46), kind=kOutput, calls=%fused_computation.42 | convolution fusion | flops 2172649472 | bytes 11534336 | tf_op jit(solution)/shard_map/dot_general | solution.py:308
  96.3 2.4 %fusion.34 = f32[256,1184]{0,1:T(8,128)S(1)} fusion(bf16[256,3584]{1,0:T(8,128)(2,1)S(1)} %bitcast.43, bf16[1184,3584]{1,0:T(8,128)(2,1)S(1)} %bitcast.46), kind=kOutput, calls=%fused_computation.41 | convolution fusion | flops 2172649472 | bytes 11534336 | tf_op jit(solution)/shard_map/dot_general | solution.py:309
  98.7 2.4 %convolution_add_fusion.1 = f32[256,1184]{0,1:T(8,128)S(1)} fusion(f32[256,1184]{0,1:T(8,128)S(1)} %fusion.34, bf16[256,3584]{1,0:T(8,128)(2,1)S(1)} %bitcast.41, bf16[1184,3584]{1,0:T(8,128)(2,1)S(1)} %bitcast.48), kind=kOutput, calls=%fused_computation.11 | convolution fusion | flops 2172952576 | bytes 12746752 | tf_op jit(solution)/shard_map/dot_general | solution.py:309
  101.1 9.2 %convolution_bitcast_fusion.1 = f32[3584,1184]{0,1:T(8,128)} fusion(bf16[256,3584]{1,0:T(8,128)(2,1)S(1)} %bitcast.36, f32[256,1184]{0,1:T(8,128)S(1)} %fusion.33, f32[256,1184]{0,1:T(8,128)S(1)} %fusion.31, f32[256,1184]{0,1:T(8,128)S(1)} %fusion.35, f32[256,1184]{0,1:T(8,128)S(1)} %fusion.32, f32[256,1184]{0,1:T(8,128)S(1)} %get-tuple-element.9, ...), kind=kOutput, calls=%fused_computation.1 | convolution fusion | flops 2179317760 | bytes 26083328 | tf_op jit(solution)/shard_map/dot_general | solution.py:24
  110.3 9.1 %convolution_bitcast_fusion = f32[3584,1184]{0,1:T(8,128)} fusion(bf16[256,3584]{1,0:T(8,128)(2,1)S(1)} %bitcast.37, f32[256,1184]{0,1:T(8,128)S(1)} %fusion.33, f32[256,1184]{0,1:T(8,128)S(1)} %fusion.35, f32[256,1184]{0,1:T(8,128)S(1)} %convolution_add_fusion.1, f32[256,1184]{0,1:T(8,128)S(1)} %fusion.31), kind=kOutput, calls=%fused_computation | convolution fusion | flops 2176589824 | bytes 23658496 | tf_op jit(solution)/shard_map/dot_general | solution.py:24
  119.4 8.6 %fusion.3 = f32[1184,3584]{1,0:T(8,128)} fusion(bf16[256,3584]{1,0:T(8,128)(2,1)S(1)} %bitcast.44, bf16[256,3584]{1,0:T(8,128)(2,1)S(1)} %bitcast.42, bf16[256,1184]{0,1:T(8,128)(2,1)S(1)} %get-tuple-element.8, bf16[256,1184]{0,1:T(8,128)(2,1)S(1)} %get-tuple-element.7), kind=kOutput, calls=%fused_computation.7 | convolution fusion | flops 4355063808 | bytes 21856256 | tf_op jit(solution)/shard_map/dot_general | solution.py:24
  (4 shorter events, 0.0 us)
Async XLA Ops:
  0.6 0.8 copy-start
  1.4 29.7 %slice-start.6 = ((s8[8486912]{0:T(1024)(128)(4,1)}), s8[4194304]{0:T(1024)(128)(4,1)S(1)}, s32[]{:S(2)}) async-start(s8[8486912]{0:T(1024)(128)(4,1)} %bitcast.49), calls=%async_computation.6 | async-start | bytes 8388608
  25.2 6.0 %slice-start.7 = ((s8[8486912]{0:T(1024)(128)(4,1)}), s8[4194304]{0:T(1024)(128)(4,1)S(1)}, s32[]{:S(2)}) async-start(s8[8486912]{0:T(1024)(128)(4,1)} %bitcast.49), calls=%async_computation.7 | async-start | bytes 8388608
  25.2 6.0 %slice-start.8 = ((s8[8486912]{0:T(1024)(128)(4,1)}), s8[98304]{0:T(1024)(128)(4,1)S(1)}, s32[]{:S(2)}) async-start(s8[8486912]{0:T(1024)(128)(4,1)} %bitcast.49), calls=%async_computation.8 | async-start | bytes 196608
  25.2 8.5 %slice-start.9 = ((s8[8486912]{0:T(1024)(128)(4,1)}), s8[4194304]{0:T(1024)(128)(4,1)S(1)}, s32[]{:S(2)}) async-start(s8[8486912]{0:T(1024)(128)(4,1)} %bitcast.51), calls=%async_computation.9 | async-start | bytes 8388608
  25.2 8.5 %slice-start.10 = ((s8[8486912]{0:T(1024)(128)(4,1)}), s8[4194304]{0:T(1024)(128)(4,1)S(1)}, s32[]{:S(2)}) async-start(s8[8486912]{0:T(1024)(128)(4,1)} %bitcast.51), calls=%async_computation.10 | async-start | bytes 8388608
  31.2 2.5 %slice-start.11 = ((s8[8486912]{0:T(1024)(128)(4,1)}), s8[98304]{0:T(1024)(128)(4,1)S(1)}, s32[]{:S(2)}) async-start(s8[8486912]{0:T(1024)(128)(4,1)} %bitcast.51), calls=%async_computation.11 | async-start | bytes 196608
  33.7 8.7 %slice-start = ((s8[8486912]{0:T(1024)(128)(4,1)}), s8[4194304]{0:T(1024)(128)(4,1)S(1)}, s32[]{:S(2)}) async-start(s8[8486912]{0:T(1024)(128)(4,1)} %bitcast.45), calls=%async_computation | async-start | bytes 8388608
  33.7 8.7 %slice-start.1 = ((s8[8486912]{0:T(1024)(128)(4,1)}), s8[4194304]{0:T(1024)(128)(4,1)S(1)}, s32[]{:S(2)}) async-start(s8[8486912]{0:T(1024)(128)(4,1)} %bitcast.45), calls=%async_computation.1 | async-start | bytes 8388608
  36.1 6.3 %slice-start.2 = ((s8[8486912]{0:T(1024)(128)(4,1)}), s8[98304]{0:T(1024)(128)(4,1)S(1)}, s32[]{:S(2)}) async-start(s8[8486912]{0:T(1024)(128)(4,1)} %bitcast.45), calls=%async_computation.2 | async-start | bytes 196608
  42.5 2.8 %slice-start.3 = ((s8[8486912]{0:T(1024)(128)(4,1)}), s8[4194304]{0:T(1024)(128)(4,1)S(1)}, s32[]{:S(2)}) async-start(s8[8486912]{0:T(1024)(128)(4,1)} %bitcast.47), calls=%async_computation.3 | async-start | bytes 8388608
  42.5 3.5 %slice-start.4 = ((s8[8486912]{0:T(1024)(128)(4,1)}), s8[4194304]{0:T(1024)(128)(4,1)S(1)}, s32[]{:S(2)}) async-start(s8[8486912]{0:T(1024)(128)(4,1)} %bitcast.47), calls=%async_computation.4 | async-start | bytes 8388608
  43.9 2.1 %slice-start.5 = ((s8[8486912]{0:T(1024)(128)(4,1)}), s8[98304]{0:T(1024)(128)(4,1)S(1)}, s32[]{:S(2)}) async-start(s8[8486912]{0:T(1024)(128)(4,1)} %bitcast.47), calls=%async_computation.5 | async-start | bytes 196608
  46.0 1.4 %copy-start.1 = (bf16[8,3584]{1,0:T(8,128)(2,1)S(1)}, bf16[8,3584]{1,0:T(8,128)(2,1)}, u32[]{:S(2)}) copy-start(bf16[8,3584]{1,0:T(8,128)(2,1)} %param.9) | copy-start | bytes 172036
